TPU v7x, 32 devices: a whole 2x2x4 slice. The times are simulated.
32 devices in a mesh: fsdp: 4 (over z), ctx: 4 (over x, core), tp: 2 (over y).
Axes of the slice: x: 2, y: 2, z: 4, core: 2. Of those that a mesh axis runs over, the one named last changes fastest.
Arguments:
- layer_in: bfloat16 [4, 1024, 1024], P('fsdp', 'ctx'), may hold values from -6 to 6
- segment_ids: int32 [4, 1024], P('fsdp', 'ctx'), may hold values from 0 to 18, as said below
- valid_mask: int32 [4, 1024], P('fsdp', 'ctx'), may hold values from 0 to 1, as said below
- teacher: bfloat16 [4, 1024, 1024], P('fsdp', 'ctx'), may hold values from -6 to 6
- attn_gain: bfloat16 [1024], P('fsdp'), may hold values from 0.099609375 to 1.8984375
- w_query: bfloat16 [1024, 256], P('fsdp', 'tp'), may hold values from -0.1875 to 0.1875
- w_key: bfloat16 [1024, 256], P('fsdp', 'tp'), may hold values from -0.1875 to 0.1875
- w_value: bfloat16 [1024, 1024], P('fsdp', 'tp'), may hold values from -0.1875 to 0.1875
- w_out: bfloat16 [1024, 1024], P('tp', 'fsdp'), may hold values from -2 to 2
- ffn_gain: bfloat16 [1024], P('fsdp'), may hold values from 0.099609375 to 1.8984375
- w_gate: bfloat16 [1024, 2752], P('fsdp', 'tp'), may hold values from -0.1875 to 0.1875
- w_up: bfloat16 [1024, 2752], P('fsdp', 'tp'), may hold values from -0.1875 to 0.1875
- w_down: bfloat16 [2752, 1024], P('tp', 'fsdp'), may hold values from -0.109375 to 0.109375
Outputs:
- layer_out: bfloat16 [4, 1024, 1024], P('fsdp', 'ctx')
- grad_in: bfloat16 [4, 1024, 1024], P('fsdp', 'ctx')
- grad_attn_gain: float32 [1024], P('fsdp')
- grad_query: float32 [1024, 256], P('fsdp', 'tp')
- grad_key: float32 [1024, 256], P('fsdp', 'tp')
- grad_value: float32 [1024, 1024], P('fsdp', 'tp')
- grad_out: float32 [1024, 1024], P('tp', 'fsdp')
- grad_ffn_gain: float32 [1024], P('fsdp')
- grad_gate: float32 [1024, 2752], P('fsdp', 'tp')
- grad_up: float32 [1024, 2752], P('fsdp', 'tp')
- grad_down: float32 [2752, 1024], P('tp', 'fsdp')
- loss_value: float32 [], replicated
Inputs may be any that keep to these rules, and one draw needn't show every extreme that they name: `segment_ids`: within each sequence the ids of valid tokens start at 0 and rise by 0 or 1 from one token to the next; equal ids in a sequence mark one document. Padding tokens carry the largest id, which no document has. `valid_mask`: in each sequence the valid tokens come first; the padding tokens after them, where there are any.
All inputs are finite; a program needn't handle non-finite values.
Results may differ from a plain program's by a relative error of at most 0.014.
Values may be sent and summed in bfloat16 or wider, within the bound.
A program may use at most 128 MiB of HBM per device.

v0:
```python
from functools import partial
import math
import jax
import jax.numpy as jnp
from jax import lax
from jax.sharding import PartitionSpec as P

FEAT = 16
HEAD_V = 64
EPSILON = 1e-05
HIGH = lax.Precision.HIGHEST
QUAD_SCALE = 1.0 / (4.0 * math.sqrt(2.0))


def entering(x, axis, join, neutral):
    place = lax.axis_index(axis)
    gathered = jax.tree.map(
        lambda a, kind: lax.all_gather(a.astype(kind), axis),
        x,
        (jnp.bfloat16, jnp.bfloat16, jnp.bfloat16),
    )
    state = jax.tree.map(lambda a, e: jnp.zeros_like(a) + jnp.asarray(e, a.dtype), x, neutral)

    def one(lap, state):
        return join(
            state,
            jax.tree.map(
                lambda a, own: lax.dynamic_index_in_dim(a, lap, 0, False).astype(own.dtype),
                gathered,
                x,
            ),
        )

    return lax.fori_loop(0, place, one, state)


def entering_2(x, axis, combine, identity):
    devices, here = (lax.axis_size(axis), lax.axis_index(axis))
    everything = jax.tree.map(
        lambda part, kind: lax.all_gather(part.astype(kind), axis),
        x,
        jax.tree.map(lambda a: jnp.bfloat16 if a.dtype == jnp.float32 else a.dtype, x),
    )
    start = jax.tree.map(
        lambda part, zero: jnp.broadcast_to(jnp.asarray(zero, part.dtype), part.shape), x, identity
    )

    def lap(k, before):
        at = devices - 1 - k
        reached = at > here
        new = combine(
            before, jax.tree.map(lambda part, own: part[at].astype(own.dtype), everything, x)
        )
        return jax.tree.map(lambda a, b: jnp.where(reached, a, b), new, before)

    return lax.fori_loop(0, devices, lap, start)


def product(left_side, right_side):
    return jnp.dot(left_side, right_side, preferred_element_type=jnp.float32)


def product_left_t(left_side, right_side):
    return lax.dot_general(
        left_side, right_side, (((0,), (0,)), ((), ())), preferred_element_type=jnp.float32
    )


def product_right_t(left_side, right_side):
    return lax.dot_general(
        left_side, right_side, (((1,), (1,)), ((), ())), preferred_element_type=jnp.float32
    )


def features(vectors):
    lead_dims = vectors.shape[:-1]
    feat_width = vectors.shape[-1]
    square = (vectors[..., :, None] * vectors[..., None, :]).reshape(
        lead_dims + (feat_width * feat_width,)
    )
    return jnp.concatenate(
        [jnp.ones(lead_dims + (1,), jnp.float32), 0.5 * vectors, QUAD_SCALE * square], axis=-1
    )


def attend(query_rows, key_rows, value_rows, prev_state, prev_norm, segment, prev_id):
    scores = jnp.einsum("slhf,smhf->shlm", query_rows, key_rows, precision=HIGH) * 0.25
    kernel = 1.0 + scores + 0.5 * scores * scores
    places = jnp.arange(segment.shape[1])
    allowed = (places[:, None] >= places[None, :])[None] & (
        segment[:, :, None] == segment[:, None, :]
    )
    kernel = jnp.where(allowed[:, None], kernel, 0.0)
    carried = (segment.astype(jnp.float32) == prev_id[:, None]).astype(jnp.float32)
    mapped = features(query_rows) * carried[:, :, None, None]
    numerator = jnp.einsum("shlm,smhv->slhv", kernel, value_rows, precision=HIGH) + jnp.einsum(
        "slht,shtv->slhv", mapped, prev_state, precision=HIGH
    )
    denominator = jnp.einsum("shlm->slh", kernel) + jnp.einsum(
        "slht,sht->slh", mapped, prev_norm, precision=HIGH
    )
    return numerator / denominator[..., None]


def summarize(key_rows, value_rows, segment):
    closing = (segment == segment[:, -1:]).astype(jnp.float32)
    mapped = features(key_rows) * closing[:, :, None, None]
    return (
        jnp.einsum("slht,slhv->shtv", mapped, value_rows, precision=HIGH),
        jnp.sum(mapped, axis=1),
    )


def rms_forward(values_in, gain_vec):
    inv_root = lax.rsqrt(jnp.mean(values_in * values_in, axis=-1, keepdims=True) + EPSILON)
    return (values_in * inv_root * gain_vec, inv_root)


def rms_backward(values_in, inv_root, gain_vec, grad_normed):
    weighted = grad_normed * gain_vec
    grad_gain = jnp.sum(grad_normed * values_in * inv_root, axis=0)
    grad_values = inv_root * weighted - values_in * inv_root**3 * jnp.mean(
        weighted * values_in, axis=-1, keepdims=True
    )
    return (grad_values, grad_gain)


def chain_combine(earlier, later):
    is_fresh = later[0] < 0
    same_doc = later[0] == earlier[0]

    def pick(early_part, late_part):
        expand = (-1,) + (1,) * (early_part.ndim - 1)
        with_early = late_part + jnp.where(same_doc.reshape(expand), early_part, 0.0)
        return jnp.where(is_fresh.reshape(expand), early_part, with_early)

    return (
        jnp.where(is_fresh, earlier[0], later[0]),
        pick(earlier[1], later[1]),
        pick(earlier[2], later[2]),
    )


def tp_forward(partial_sum):
    return lax.psum(partial_sum, "tp")


def tp_backward(partial_sum):
    return lax.psum(partial_sum.astype(jnp.bfloat16), "tp").astype(jnp.float32)


def per_device(
    layer_in,
    segment_ids,
    valid_mask,
    teacher,
    attn_gain,
    w_query,
    w_key,
    w_value,
    w_out,
    ffn_gain,
    w_gate,
    w_up,
    w_down,
):
    full_weights = (
        lax.all_gather(attn_gain, "fsdp", axis=0, tiled=True),
        lax.all_gather(w_query, "fsdp", axis=0, tiled=True),
        lax.all_gather(w_key, "fsdp", axis=0, tiled=True),
        lax.all_gather(w_value, "fsdp", axis=0, tiled=True),
        lax.all_gather(w_out, "fsdp", axis=1, tiled=True),
        lax.all_gather(ffn_gain, "fsdp", axis=0, tiled=True),
        lax.all_gather(w_gate, "fsdp", axis=0, tiled=True),
        lax.all_gather(w_up, "fsdp", axis=0, tiled=True),
        lax.all_gather(w_down, "fsdp", axis=1, tiled=True),
    )
    (
        gain_one,
        full_query,
        full_key,
        full_value,
        full_out,
        gain_two,
        full_gate,
        full_up,
        full_down,
    ) = full_weights
    seq_count, shard_len, model_width = layer_in.shape
    row_count = seq_count * shard_len
    heads_here = full_query.shape[1] // FEAT
    rows_in = layer_in.reshape(row_count, model_width).astype(jnp.float32)
    normed_full, root_one = rms_forward(rows_in, gain_one.astype(jnp.float32))
    normed_one = normed_full.astype(jnp.bfloat16)
    query_rows = product(normed_one, full_query).reshape(seq_count, shard_len, heads_here, FEAT)
    key_rows = product(normed_one, full_key).reshape(seq_count, shard_len, heads_here, FEAT)
    value_rows = product(normed_one, full_value).reshape(seq_count, shard_len, heads_here, HEAD_V)
    last_id = segment_ids[:, -1].astype(jnp.float32)
    first_id = segment_ids[:, 0].astype(jnp.float32)
    (out_state, out_norm), summary_pull = jax.vjp(
        partial(summarize, segment=segment_ids), key_rows, value_rows
    )
    blank_state = jnp.zeros_like(out_state)
    blank_norm = jnp.zeros_like(out_norm)
    no_doc = jnp.full_like(last_id, -1.0)
    prev_id, prev_state, prev_norm = entering(
        (last_id, out_state, out_norm), "ctx", chain_combine, (no_doc, blank_state, blank_norm)
    )
    attended, attend_pull = jax.vjp(
        partial(attend, segment=segment_ids, prev_id=prev_id),
        query_rows,
        key_rows,
        value_rows,
        prev_state,
        prev_norm,
    )
    mixed_heads = attended.reshape(row_count, heads_here * HEAD_V).astype(jnp.bfloat16)
    head_sum = product(mixed_heads, full_out)
    teacher_rows = teacher.reshape(row_count, model_width).astype(jnp.float32)
    weight_rows = valid_mask.reshape(row_count, 1).astype(jnp.float32)
    middle = rows_in + tp_forward(head_sum)
    normed_mid, root_two = rms_forward(middle, gain_two.astype(jnp.float32))
    normed_two = normed_mid.astype(jnp.bfloat16)
    gate_rows = product(normed_two, full_gate)
    up_rows = product(normed_two, full_up)
    sigmoid_gate = jax.nn.sigmoid(gate_rows)
    silu_gate = gate_rows * sigmoid_gate
    hidden = (silu_gate * up_rows).astype(jnp.bfloat16)
    down_sum = product(hidden, full_down)
    output = middle + tp_forward(down_sum)
    misfit = (output - teacher_rows) * weight_rows
    layer_rows = output.astype(jnp.bfloat16)
    grad_rows = misfit.astype(jnp.bfloat16)
    sum_squares = jnp.sum(misfit * misfit)
    sum_valid = jnp.sum(weight_rows)
    back_weights = (
        lax.all_gather(attn_gain, "fsdp", axis=0, tiled=True),
        lax.all_gather(w_query, "fsdp", axis=0, tiled=True),
        lax.all_gather(w_key, "fsdp", axis=0, tiled=True),
        lax.all_gather(w_value, "fsdp", axis=0, tiled=True),
        lax.all_gather(w_out, "fsdp", axis=1, tiled=True),
        lax.all_gather(ffn_gain, "fsdp", axis=0, tiled=True),
        lax.all_gather(w_gate, "fsdp", axis=0, tiled=True),
        lax.all_gather(w_up, "fsdp", axis=0, tiled=True),
        lax.all_gather(w_down, "fsdp", axis=1, tiled=True),
    )
    (
        gain_one,
        full_query,
        full_key,
        full_value,
        full_out,
        gain_two,
        full_gate,
        full_up,
        full_down,
    ) = back_weights
    grad_down = product_left_t(hidden, grad_rows)
    grad_hidden = product_right_t(grad_rows, full_down)
    grad_gate_rows = (
        grad_hidden * up_rows * sigmoid_gate * (1.0 + gate_rows * (1.0 - sigmoid_gate))
    ).astype(jnp.bfloat16)
    grad_up_rows = (grad_hidden * silu_gate).astype(jnp.bfloat16)
    grad_gate = product_left_t(normed_two, grad_gate_rows)
    grad_up = product_left_t(normed_two, grad_up_rows)
    normed_two_terms = product_right_t(grad_gate_rows, full_gate) + product_right_t(
        grad_up_rows, full_up
    )
    grad_normed_two = tp_backward(normed_two_terms)
    grad_mid_norm, grad_ffn_gain = rms_backward(
        middle, root_two, gain_two.astype(jnp.float32), grad_normed_two
    )
    grad_middle = misfit + grad_mid_norm
    grad_branch = grad_middle.astype(jnp.bfloat16)
    grad_out = product_left_t(mixed_heads, grad_branch)
    grad_mixed = product_right_t(grad_branch, full_out).reshape(
        seq_count, shard_len, heads_here, HEAD_V
    )
    grad_q_near, grad_k_near, grad_v_near, grad_prev_state, grad_prev_norm = attend_pull(grad_mixed)
    next_id, later_state, later_norm = entering_2(
        (first_id, grad_prev_state, grad_prev_norm),
        "ctx",
        chain_combine,
        (no_doc, blank_state, blank_norm),
    )
    continues = (next_id == last_id).astype(jnp.float32)
    grad_k_far, grad_v_far = summary_pull(
        (later_state * continues[:, None, None, None], later_norm * continues[:, None, None])
    )
    grad_query_rows = grad_q_near.reshape(row_count, heads_here * FEAT).astype(jnp.bfloat16)
    grad_key_rows = (
        (grad_k_near + grad_k_far).reshape(row_count, heads_here * FEAT).astype(jnp.bfloat16)
    )
    grad_value_rows = (
        (grad_v_near + grad_v_far).reshape(row_count, heads_here * HEAD_V).astype(jnp.bfloat16)
    )
    grad_query = product_left_t(normed_one, grad_query_rows)
    grad_key = product_left_t(normed_one, grad_key_rows)
    grad_value = product_left_t(normed_one, grad_value_rows)
    normed_one_terms = (
        product_right_t(grad_query_rows, full_query)
        + product_right_t(grad_key_rows, full_key)
        + product_right_t(grad_value_rows, full_value)
    )
    grad_normed_one = tp_backward(normed_one_terms)
    grad_rows_in, grad_attn_gain = rms_backward(
        rows_in, root_one, gain_one.astype(jnp.float32), grad_normed_one
    )
    grad_in_rows = (grad_middle + grad_rows_in).astype(jnp.bfloat16)
    total_sq, total_valid = lax.psum((sum_squares, sum_valid), ("fsdp", "ctx"))
    loss_value = total_sq / (total_valid * model_width)
    grad_in = grad_in_rows.reshape(seq_count, shard_len, model_width)
    layer_out = layer_rows.reshape(seq_count, shard_len, model_width)
    owned = (
        lax.psum_scatter(
            grad_attn_gain.astype(jnp.bfloat16), "fsdp", scatter_dimension=0, tiled=True
        ).astype(jnp.float32),
        lax.psum_scatter(
            grad_query.astype(jnp.bfloat16), "fsdp", scatter_dimension=0, tiled=True
        ).astype(jnp.float32),
        lax.psum_scatter(
            grad_key.astype(jnp.bfloat16), "fsdp", scatter_dimension=0, tiled=True
        ).astype(jnp.float32),
        lax.psum_scatter(
            grad_value.astype(jnp.bfloat16), "fsdp", scatter_dimension=0, tiled=True
        ).astype(jnp.float32),
        lax.psum_scatter(
            grad_out.astype(jnp.bfloat16), "fsdp", scatter_dimension=1, tiled=True
        ).astype(jnp.float32),
        lax.psum_scatter(
            grad_ffn_gain.astype(jnp.bfloat16), "fsdp", scatter_dimension=0, tiled=True
        ).astype(jnp.float32),
        lax.psum_scatter(
            grad_gate.astype(jnp.bfloat16), "fsdp", scatter_dimension=0, tiled=True
        ).astype(jnp.float32),
        lax.psum_scatter(
            grad_up.astype(jnp.bfloat16), "fsdp", scatter_dimension=0, tiled=True
        ).astype(jnp.float32),
        lax.psum_scatter(
            grad_down.astype(jnp.bfloat16), "fsdp", scatter_dimension=1, tiled=True
        ).astype(jnp.float32),
    )
    shares = (
        lax.psum(owned[0].astype(jnp.bfloat16), "ctx").astype(jnp.float32),
        lax.psum(owned[1].astype(jnp.bfloat16), "ctx").astype(jnp.float32),
        lax.psum(owned[2].astype(jnp.bfloat16), "ctx").astype(jnp.float32),
        lax.psum(owned[3].astype(jnp.bfloat16), "ctx").astype(jnp.float32),
        lax.psum(owned[4].astype(jnp.bfloat16), "ctx").astype(jnp.float32),
        lax.psum(owned[5].astype(jnp.bfloat16), "ctx").astype(jnp.float32),
        lax.psum(owned[6].astype(jnp.bfloat16), "ctx").astype(jnp.float32),
        lax.psum(owned[7].astype(jnp.bfloat16), "ctx").astype(jnp.float32),
        lax.psum(owned[8].astype(jnp.bfloat16), "ctx").astype(jnp.float32),
    )
    return (
        layer_out,
        grad_in,
        shares[0],
        shares[1],
        shares[2],
        shares[3],
        shares[4],
        shares[5],
        shares[6],
        shares[7],
        shares[8],
        loss_value,
    )


def solution(mesh):
    placed = (
        P("fsdp", "ctx", None),
        P("fsdp", "ctx"),
        P("fsdp", "ctx"),
        P("fsdp", "ctx", None),
        P("fsdp"),
        P("fsdp", "tp"),
        P("fsdp", "tp"),
        P("fsdp", "tp"),
        P("tp", "fsdp"),
        P("fsdp"),
        P("fsdp", "tp"),
        P("fsdp", "tp"),
        P("tp", "fsdp"),
    )
    return jax.shard_map(
        per_device,
        mesh=mesh,
        in_specs=placed,
        out_specs=(
            P("fsdp", "ctx", None),
            P("fsdp", "ctx", None),
            P("fsdp"),
            P("fsdp", "tp"),
            P("fsdp", "tp"),
            P("fsdp", "tp"),
            P("tp", "fsdp"),
            P("fsdp"),
            P("fsdp", "tp"),
            P("fsdp", "tp"),
            P("tp", "fsdp"),
            P(),
        ),
        check_vma=False,
    )
```

profile of v0, /device:TPU:0, one launch (start us, length us, event | category | flops | bytes accessed | tf_op | source)
XLA Modules:
  0.0 834.6 jit_solution(4206275548353771715)
XLA Ops:
  8.6 12.6 %all-gather.5 = bf16[4,1,256]{2,1,0:T(2,128)(2,1)S(1)} all-gather(bf16[1,1,256]{2,1,0:T(2,128)(2,1)S(1)} %reshape.818), channel_id=1, replica_groups=mesh['fsdp'=4,'ctx'=4,'tp'=2] {'fsdp'}, dimensions={0}, use_global_device_ids=true | all-gather | bytes 2560 | tf_op jit(solution)/shard_map/all_gather | solution.py:168
  21.3 16.3 %all_gather.71 = bf16[1024,128]{1,0:T(8,128)(2,1)S(1)} all-gather(bf16[256,128]{1,0:T(8,128)(2,1)} %param.23), channel_id=1, replica_groups=mesh['fsdp'=4,'ctx'=4,'tp'=2] {'fsdp'}, dimensions={0}, use_global_device_ids=true | all-gather | bytes 327680 | tf_op jit(solution)/shard_map/all_gather | solution.py:170
  55.8 5.2 all-gather.2
  62.2 14.5 %all_gather.70 = bf16[1024,128]{1,0:T(8,128)(2,1)S(1)} all-gather(bf16[256,128]{1,0:T(8,128)(2,1)S(1)} %copy-done.48), channel_id=1, replica_groups=mesh['fsdp'=4,'ctx'=4,'tp'=2] {'fsdp'}, dimensions={0}, use_global_device_ids=true | all-gather | bytes 327680 | tf_op jit(solution)/shard_map/all_gather | solution.py:169
  85.4 6.5 all-reduce.6
  107.5 10.1 %all-gather.6 = bf16[4,1,256]{2,1,0:T(2,128)(2,1)S(1)} all-gather(bf16[1,1,256]{2,1,0:T(2,128)(2,1)S(1)} %reshape.820), channel_id=1, replica_groups=mesh['fsdp'=4,'ctx'=4,'tp'=2] {'fsdp'}, dimensions={0}, use_global_device_ids=true | all-gather | bytes 2560 | tf_op jit(solution)/shard_map/all_gather | solution.py:173
  117.7 38.3 %all-reduce.15.cloned.1.call-done = f32[256,1024]{1,0:T(8,128)} async-done(((f32[256,1024]{1,0:T(8,128)}), f32[256,1024]{1,0:T(8,128)}) %all-reduce.15.cloned.1.call-update) | async-done | bytes 1048592 | tf_op jit(solution)/shard_map/psum | solution.py:145
  157.6 57.8 %all-gather.19.cloned.1.call-done = bf16[1024,1376]{0,1:T(8,128)(2,1)} async-done(((bf16[256,1376]{0,1:T(8,128)(2,1)}), bf16[1024,1376]{0,1:T(8,128)(2,1)}) %all-gather.19.cloned.1.call-update) | async-done | bytes 2818064 | tf_op jit(solution)/shard_map/all_gather | solution.py:174
  219.2 53.9 %all-gather.21.cloned.1.call-done = bf16[1024,1376]{0,1:T(8,128)(2,1)} async-done(((bf16[256,1376]{0,1:T(8,128)(2,1)}), bf16[1024,1376]{0,1:T(8,128)(2,1)}) %all-gather.21.cloned.1.call-update) | async-done | bytes 2818064 | tf_op jit(solution)/shard_map/all_gather | solution.py:175
  277.7 53.2 %all-gather.23.cloned.1.call-done = bf16[1376,1024]{1,0:T(8,128)(2,1)} async-done(((bf16[1376,256]{1,0:T(8,128)(2,1)}), bf16[1376,1024]{1,0:T(8,128)(2,1)}) %all-gather.23.cloned.1.call-update) | async-done | bytes 2818064 | tf_op jit(solution)/shard_map/all_gather | solution.py:176
  335.0 38.4 %all-reduce.17.cloned.1.call-done = f32[256,1024]{1,0:T(8,128)} async-done(((f32[256,1024]{1,0:T(8,128)}), f32[256,1024]{1,0:T(8,128)}) %all-reduce.17.cloned.1.call-update) | async-done | bytes 1048592 | tf_op jit(solution)/shard_map/psum | solution.py:145
  384.3 10.9 %all-gather.27.cloned.1.call-start = ((), (), s32[]{:S(2)}) async-start(), calls=%async_computation.24 | async-start | bytes 1966080 | tf_op jit(solution)/shard_map/all_gather | solution.py:40
  395.2 17.9 %all-reduce.19.cloned.1.call-done = bf16[256,1024]{1,0:T(8,128)(2,1)} async-done(((bf16[256,1024]{1,0:T(8,128)(2,1)}), bf16[256,1024]{1,0:T(8,128)(2,1)}) %all-reduce.19.cloned.1.call-update) | async-done | bytes 524304 | tf_op jit(solution)/shard_map/psum | solution.py:149
  426.3 5.2 all-gather.4
  451.4 18.1 %while.35 = (s32[]{:T(128)}, f32[1]{0:T(128)}, f32[1,8,273,64]{3,2,1,0:T(8,128)S(1)}, f32[1,8,273]{2,1,0:T(8,128)S(1)}, s32[]{:T(128)}, /*index=5*/bf16[4,1]{0,1...) while((s32[]{:T(128)}, f32[1]{0:T(128)}, ...), condition=%wide.region_14.15_spmd.clone, body=%wide.region_13.14_spmd.clone.sunk | while | flops 851772 | bytes 2538059 | solution.py:56
  501.9 21.3 %reduce-scatter.10.cloned.1.call-done = bf16[256,128]{1,0:T(8,128)(2,1)} async-done(((bf16[1024,128]{1,0:T(8,128)(2,1)}), bf16[256,128]{1,0:T(8,128)(2,1)}) %reduce-scatter.10.cloned.1.call-update) | async-done | bytes 65552 | tf_op jit(solution)/shard_map/reduce_scatter | solution.py:321
  523.3 28.3 %reduce-scatter.12.cloned.1.call-done = bf16[256,512]{1,0:T(8,128)(2,1)} async-done(((bf16[1024,512]{1,0:T(8,128)(2,1)}), bf16[256,512]{1,0:T(8,128)(2,1)}) %reduce-scatter.12.cloned.1.call-update) | async-done | bytes 262160 | tf_op jit(solution)/shard_map/reduce_scatter | solution.py:324
  551.6 56.0 %reduce-scatter.20.cloned.1.call-done = bf16[1376,256]{1,0:T(8,128)(2,1)} async-done(((bf16[1376,1024]{1,0:T(8,128)(2,1)}), bf16[1376,256]{1,0:T(8,128)(2,1)}) %reduce-scatter.20.cloned.1.call-update) | async-done | bytes 704528 | tf_op jit(solution)/shard_map/reduce_scatter | solution.py:339
  607.5 57.2 %reduce-scatter.16.cloned.1.call-done = bf16[256,1376]{0,1:T(8,128)(2,1)} async-done(((bf16[1024,1376]{0,1:T(8,128)(2,1)}), bf16[256,1376]{0,1:T(8,128)(2,1)}) %reduce-scatter.16.cloned.1.call-update) | async-done | bytes 704528 | tf_op jit(solution)/shard_map/reduce_scatter | solution.py:333
  664.7 57.2 %reduce-scatter.18.cloned.1.call-done = bf16[256,1376]{0,1:T(8,128)(2,1)} async-done(((bf16[1024,1376]{0,1:T(8,128)(2,1)}), bf16[256,1376]{0,1:T(8,128)(2,1)}) %reduce-scatter.18.cloned.1.call-update) | async-done | bytes 704528 | tf_op jit(solution)/shard_map/reduce_scatter | solution.py:336
  723.8 32.4 %all-reduce.4 = (f32[]{:T(128)}, f32[]{:T(128)}) all-reduce(f32[]{:T(128)} %get-tuple-element.377, f32[]{:T(128)} %convert_reduce_fusion), channel_id=1, replica_groups=mesh['fsdp'=4,'ctx'=4,'tp'=2] {'fsdp','ctx'}, use_global_device_ids=true, to_apply=%region_40.41 | all-reduce | flops 2 | bytes 16 | tf_op jit(solution)/shard_map/psum | solution.py:310
  758.9 8.4 %all-reduce.8 = (bf16[1024]{0:T(1024)(128)(2,1)S(1)}, bf16[1024]{0:T(1024)(128)(2,1)S(1)}) all-reduce(bf16[1024]{0:T(1024)(128)(2,1)S(1)} %get-tuple-element.328, bf16[1024]{0:T(1024)(128)(2,1)S(1)} %copy-done.55), channel_id=7, replica_groups=mesh['fsdp'=4,'ctx'=4,'tp'=2] {'fsdp'}, use_global_device_ids=true, to_apply=%region_20.21.clone | all-reduce | flops 2048 | bytes 8192
  767.5 6.3 all-reduce.5
  777.1 41.5 %all-reduce.23.cloned.1.call-done = (bf16[256,128]{1,0:T(8,128)(2,1)}, bf16[256,128]{1,0:T(8,128)(2,1)}, bf16[256,512]{1,0:T(8,128)(2,1)}, bf16[512,256]{1,0:T(8...) async-done(((bf16[256,128]{1,0:T(8,128)(2,1)}, bf16[256,128]{1,0:T(8,128)(2,1)}, bf16[256,512]{1,0:T(8,128)(2,1)}, ...) | async-done | bytes 2768912 | tf_op jit(solution)/shard_map/psum | solution.py:345
  (303 shorter events, 157.4 us)
Async XLA Ops:
  7.2 37.4 %all-gather.15.cloned.1.call-start = ((), (), s32[]{:S(2)}) async-start(), calls=%async_computation.7 | async-start | bytes 1310720 | tf_op jit(solution)/shard_map/all_gather | solution.py:171
  7.9 86.6 %all-gather.25.cloned.1.call-start = ((), (), s32[]{:S(2)}) async-start(), calls=%async_computation.23 | async-start | bytes 1966080 | tf_op jit(solution)/shard_map/all_gather | solution.py:18
  52.8 49.9 %all-gather.17.cloned.1.call-start = ((), (), s32[]{:S(2)}) async-start(), calls=%async_computation.8 | async-start | bytes 1310720 | tf_op jit(solution)/shard_map/all_gather | solution.py:172
  53.6 102.4 %all-reduce.15.cloned.1.call-start = ((), (), s32[]{:S(2)}) async-start(), calls=%async_computation.9 | async-start | bytes 2097152 | tf_op jit(solution)/shard_map/psum | solution.py:145
  95.0 327.6 %copy-start.57 = (f32[1,256]{1,0:T(1,128)}, f32[1,256]{1,0:T(1,128)S(1)}, u32[]{:S(2)}) copy-start(f32[1,256]{1,0:T(1,128)S(1)} %compare_convert_fusion) | copy-start | bytes 3076
  105.6 109.9 %all-gather.19.cloned.1.call-start = ((), (), s32[]{:S(2)}) async-start(), calls=%async_computation.10 | async-start | bytes 3522560 | tf_op jit(solution)/shard_map/all_gather | solution.py:174
  106.1 167.0 %all-gather.21.cloned.1.call-start = ((), (), s32[]{:S(2)}) async-start(), calls=%async_computation.11 | async-start | bytes 3522560 | tf_op jit(solution)/shard_map/all_gather | solution.py:175
  106.7 224.2 %all-gather.23.cloned.1.call-start = ((), (), s32[]{:S(2)}) async-start(), calls=%async_computation.12 | async-start | bytes 3522560 | tf_op jit(solution)/shard_map/all_gather | solution.py:176
  107.5 265.9 %all-reduce.17.cloned.1.call-start = ((), (), s32[]{:S(2)}) async-start(), calls=%async_computation.13 | async-start | bytes 2097152 | tf_op jit(solution)/shard_map/psum | solution.py:145
  335.0 78.1 %all-reduce.19.cloned.1.call-start = ((), (), s32[]{:S(2)}) async-start(), calls=%async_computation.14 | async-start | bytes 1048576 | tf_op jit(solution)/shard_map/psum | solution.py:149
  384.3 67.1 %all-gather.27.cloned.1.call-start = ((), (), s32[]{:S(2)}) async-start(), calls=%async_computation.24 | async-start | bytes 1966080 | tf_op jit(solution)/shard_map/all_gather | solution.py:40
  431.6 66.1 %reduce-scatter.8.cloned.1.call-start = ((), (), s32[]{:S(2)}) async-start(), calls=%async_computation.16 | async-start | bytes 327680 | tf_op jit(solution)/shard_map/reduce_scatter | solution.py:318
  442.0 60.0 %reduce-scatter.14.cloned.1.call-start = ((), (), s32[]{:S(2)}) async-start(), calls=%async_computation.19 | async-start | bytes 1310720 | tf_op jit(solution)/shard_map/reduce_scatter | solution.py:327
  448.3 75.0 %reduce-scatter.10.cloned.1.call-start = ((), (), s32[]{:S(2)}) async-start(), calls=%async_computation.17 | async-start | bytes 327680 | tf_op jit(solution)/shard_map/reduce_scatter | solution.py:321
  477.5 74.0 %reduce-scatter.12.cloned.1.call-start = ((), (), s32[]{:S(2)}) async-start(), calls=%async_computation.18 | async-start | bytes 1310720 | tf_op jit(solution)/shard_map/reduce_scatter | solution.py:324
  484.2 123.3 %reduce-scatter.20.cloned.1.call-start = ((), (), s32[]{:S(2)}) async-start(), calls=%async_computation.22 | async-start | bytes 3522560 | tf_op jit(solution)/shard_map/reduce_scatter | solution.py:339
  486.7 178.0 %reduce-scatter.16.cloned.1.call-start = ((), (), s32[]{:S(2)}) async-start(), calls=%async_computation.20 | async-start | bytes 3522560 | tf_op jit(solution)/shard_map/reduce_scatter | solution.py:333
  490.5 231.5 %reduce-scatter.18.cloned.1.call-start = ((), (), s32[]{:S(2)}) async-start(), calls=%async_computation.21 | async-start | bytes 3522560 | tf_op jit(solution)/shard_map/reduce_scatter | solution.py:336
  494.1 263.4 %all-reduce.21.cloned.1.call-start = ((), (), s32[]{:S(2)}) async-start(), calls=%async_computation.15 | async-start | bytes 1048576 | tf_op jit(solution)/shard_map/psum | solution.py:149
  497.6 224.4 %copy-start.62 = (u32[32]{0:T(128)S(1)}, u32[32]{0:T(128)}, u32[]{:S(2)}) copy-start(u32[32]{0:T(128)} %constant.137) | copy-start | bytes 388
  497.6 225.6 %copy-start.59 = (s32[1,256]{1,0:T(1,128)S(1)}, s32[1,256]{1,0:T(1,128)}, u32[]{:S(2)}) copy-start(s32[1,256]{1,0:T(1,128)} %param.19) | copy-start | bytes 3076
  497.6 261.4 %copy-start.55 = (bf16[1024]{0:T(1024)(128)(2,1)S(1)}, bf16[1024]{0:T(1024)(128)(2,1)}, u32[]{:S(2)}) copy-start(bf16[1024]{0:T(1024)(128)(2,1)} %get-tuple-element.326) | copy-start | bytes 6148
  497.6 277.4 %copy-start.56 = (f32[256]{0:T(256)S(1)}, f32[256]{0:T(256)}, u32[]{:S(2)}) copy-start(f32[256]{0:T(256)} %get-tuple-element.390) | copy-start | bytes 3076
  497.6 321.0 %all-reduce.23.cloned.1.call-start = ((), (), s32[]{:S(2)}) async-start(), calls=%async_computation.25 | async-start | bytes 5537792 | tf_op jit(solution)/shard_map/psum | solution.py:345
  (66 other events, 390.1 us)
Sparse Core Ops, SparseCore 0:
  9.6 34.3 all-gather.14
  53.0 18.2 all-gather.24
  72.8 29.9 all-gather.16
  105.7 50.2 all-reduce.14
  157.4 58.0 all-gather.18
  216.8 56.2 all-gather.20
  274.7 56.2 all-gather.22
  335.1 38.2 all-reduce.16
  384.4 28.6 all-reduce.18
  431.7 19.6 all-gather.26
  453.6 19.9 reduce-scatter.7
  476.4 25.5 reduce-scatter.13
  504.8 18.4 reduce-scatter.9
  526.0 25.5 reduce-scatter.11
  553.7 53.7 reduce-scatter.19
  609.7 54.9 reduce-scatter.15
  666.9 54.9 reduce-scatter.17
  724.6 28.3 all-reduce.20
  755.9 62.6 all-reduce.22
where the time goes:
time: 844 us; the launch traced here: 835 us
  waiting for transfers between devices  532 us (63%)
  blocking collectives  118 us (14%)
  matrix products  83.8 us (10%)
  other arithmetic  33.4 us (4%)
  local copies, waits for them, and re-layouts  27.4 us (3%)
  between operations  19.7 us (2%)
  starting transfers between devices  12.1 us (1%)
    psum x2, waiting for transfers between devices, tp_forward(): return lax.psum(partial_sum, 'tp')  76.7 us
    all_gather x1, waiting for transfers between devices, per_device(): lax.all_gather(w_gate, 'fsdp', axis=0, tiled=True)  57.8 us
    reduce_scatter x1, waiting for transfers between devices, per_device(): lax.psum_scatter(grad_gate.astype(jnp.bfloat16), 'fsdp', scatter_dimensio...  57.2 us
    reduce_scatter x1, waiting for transfers between devices, per_device(): lax.psum_scatter(grad_up.astype(jnp.bfloat16), 'fsdp', scatter_dimension=...  57.2 us
    reduce_scatter x1, waiting for transfers between devices, per_device(): lax.psum_scatter(grad_down.astype(jnp.bfloat16), 'fsdp', scatter_dimensio...  56 us
    all_gather x1, waiting for transfers between devices, per_device(): lax.all_gather(w_up, 'fsdp', axis=0, tiled=True)  53.9 us
    all_gather x1, waiting for transfers between devices, per_device(): lax.all_gather(w_down, 'fsdp', axis=1, tiled=True)  53.2 us
    psum x1, waiting for transfers between devices, per_device(): lax.psum(owned[1].astype(jnp.bfloat16), 'ctx').astype(jnp.float32)  41.5 us
  transfers between devices with their start and end apart: 19, of which 15 were waited for; matrix products, arithmetic and copies ran while one was open for 11% of the time, Pallas kernels for 0%

commit v1 on v0

--- a/solution.py
+++ b/solution.py
@@ -10,6 +10,28 @@
 EPSILON = 1e-05
 HIGH = lax.Precision.HIGHEST
 QUAD_SCALE = 1.0 / (4.0 * math.sqrt(2.0))
+
+
+def joined_along(tiles, dim):
+    tiles = jnp.moveaxis(tiles, 0, dim)
+    dims = tiles.shape
+    return tiles.reshape(*dims[:dim], dims[dim] * dims[dim + 1], *dims[dim + 2 :])
+
+
+def gather_around(x, axis, dim):
+    size = lax.axis_size(axis)
+    pairs = [(i, (i + 1) % size) for i in range(size)]
+    back = [(b, a) for a, b in pairs]
+    lower, upper = ([], [])
+    for step in range(size - 1):
+        if step % 2 == 0:
+            lower.append(lax.ppermute(lower[-1] if lower else x, axis, pairs))
+        else:
+            upper.append(lax.ppermute(upper[-1] if upper else x, axis, back))
+    blocks = jnp.stack([*lower[::-1], x, *upper])
+    shift = lax.axis_index(axis) - len(lower)
+    blocks = blocks[(jnp.arange(size) - shift) % size]
+    return joined_along(blocks, dim)
 
 
 def entering(x, axis, join, neutral):
@@ -173,7 +195,7 @@
         lax.all_gather(ffn_gain, "fsdp", axis=0, tiled=True),
         lax.all_gather(w_gate, "fsdp", axis=0, tiled=True),
         lax.all_gather(w_up, "fsdp", axis=0, tiled=True),
-        lax.all_gather(w_down, "fsdp", axis=1, tiled=True),
+        gather_around(w_down, "fsdp", 1),
     )
     (
         gain_one,

time: 844 us -> 845 us (level)
  waiting for transfers between devices: 532 us -> 493 us
  blocking collectives: 118 us -> 141 us
  local copies, waits for them, and re-layouts: 27.4 us -> 37 us
    psum x2, waiting for transfers between devices: 76.7 us -> 37.6 us  [tp_forward(): return lax.psum(partial_sum, 'tp')]
    all_gather x1, blocking collectives: 10.1 us -> 33.6 us  [per_device(): lax.all_gather(ffn_gain, 'fsdp', axis=0, tiled=True)]
    all_gather x1, waiting for transfers between devices: 57.8 us -> 40.6 us  [per_device(): lax.all_gather(w_gate, 'fsdp', axis=0, tiled=True)]
    ppermute x0 -> x3, waiting for transfers between devices: none -> 14.9 us  [the longest x2 14.9 us: gather_around(): lower.append(lax.ppermute(lower[-1] if lower else x, axis, pairs))]
  transfers between devices with their start and end apart: 19 -> 22, of which waited for: 15 -> 15; matrix products, arithmetic and copies ran while one was open for 11% -> 12% of each run, Pallas kernels for 0% -> 0%
where the time goes in v1:
time: 845 us; the launch traced here: 835 us
  waiting for transfers between devices  493 us (58%)
  blocking collectives  141 us (17%)
  matrix products  82.3 us (10%)
  local copies, waits for them, and re-layouts  37 us (4%)
  other arithmetic  36 us (4%)
  between operations  19.7 us (2%)
  starting transfers between devices  18.4 us (2%)
    reduce_scatter x1, waiting for transfers between devices, per_device(): lax.psum_scatter(grad_gate.astype(jnp.bfloat16), 'fsdp', scatter_dimensio...  57.2 us
    reduce_scatter x1, waiting for transfers between devices, per_device(): lax.psum_scatter(grad_up.astype(jnp.bfloat16), 'fsdp', scatter_dimension=...  57.2 us
    all_gather x1, waiting for transfers between devices, per_device(): lax.all_gather(w_down, 'fsdp', axis=1, tiled=True)  56.6 us
    reduce_scatter x1, waiting for transfers between devices, per_device(): lax.psum_scatter(grad_down.astype(jnp.bfloat16), 'fsdp', scatter_dimensio...  56 us
    all_gather x1, waiting for transfers between devices, per_device(): lax.all_gather(w_up, 'fsdp', axis=0, tiled=True)  53.9 us
    psum x1, waiting for transfers between devices, per_device(): lax.psum(owned[1].astype(jnp.bfloat16), 'ctx').astype(jnp.float32)  41.5 us
    all_gather x1, waiting for transfers between devices, per_device(): lax.all_gather(w_gate, 'fsdp', axis=0, tiled=True)  40.6 us
    psum x2, waiting for transfers between devices, tp_forward(): return lax.psum(partial_sum, 'tp')  37.6 us
  transfers between devices with their start and end apart: 22, of which 15 were waited for; matrix products, arithmetic and copies ran while one was open for 12% of the time, Pallas kernels for 0%

profile of v1, /device:TPU:0, one launch (start us, length us, event | category | flops | bytes accessed | tf_op | source)
XLA Modules:
  0.0 835.3 jit_solution(6911296357711737349)
XLA Ops:
  8.6 12.6 %all-gather.5 = bf16[4,1,256]{2,1,0:T(2,128)(2,1)S(1)} all-gather(bf16[1,1,256]{2,1,0:T(2,128)(2,1)S(1)} %reshape.879), channel_id=1, replica_groups=mesh['fsdp'=4,'ctx'=4,'tp'=2] {'fsdp'}, dimensions={0}, use_global_device_ids=true | all-gather | bytes 2560 | tf_op jit(solution)/shard_map/all_gather | solution.py:190
  21.3 16.3 %all_gather.70 = bf16[1024,128]{1,0:T(8,128)(2,1)S(1)} all-gather(bf16[256,128]{1,0:T(8,128)(2,1)} %param.23), channel_id=1, replica_groups=mesh['fsdp'=4,'ctx'=4,'tp'=2] {'fsdp'}, dimensions={0}, use_global_device_ids=true | all-gather | bytes 327680 | tf_op jit(solution)/shard_map/all_gather | solution.py:192
  55.8 5.2 all-gather.2
  62.2 14.5 %all_gather.69 = bf16[1024,128]{1,0:T(8,128)(2,1)S(1)} all-gather(bf16[256,128]{1,0:T(8,128)(2,1)S(1)} %copy-done.50), channel_id=1, replica_groups=mesh['fsdp'=4,'ctx'=4,'tp'=2] {'fsdp'}, dimensions={0}, use_global_device_ids=true | all-gather | bytes 327680 | tf_op jit(solution)/shard_map/all_gather | solution.py:191
  85.4 6.6 all-reduce.6
  110.7 14.9 %collective-permute-done = bf16[1376,256]{1,0:T(8,128)(2,1)S(1)} collective-permute-done((bf16[1376,256]{1,0:T(8,128)(2,1)S(1)}, bf16[1376,256]{1,0:T(8,128)(2,1)S(1)}, u32[]{:S(2)}, u32[]{:S(2)}) %collective-permute-start) | collective-permute-done | bytes 704544 | tf_op jit(solution)/shard_map/ppermute | solution.py:28
  128.1 33.6 %all-gather.6 = bf16[4,1,256]{2,1,0:T(2,128)(2,1)S(1)} all-gather(bf16[1,1,256]{2,1,0:T(2,128)(2,1)S(1)} %reshape.881), channel_id=1, replica_groups=mesh['fsdp'=4,'ctx'=4,'tp'=2] {'fsdp'}, dimensions={0}, use_global_device_ids=true | all-gather | bytes 2560 | tf_op jit(solution)/shard_map/all_gather | solution.py:195
  174.9 40.6 %all-gather.19.cloned.1.call-done = bf16[1024,1376]{0,1:T(8,128)(2,1)} async-done(((bf16[256,1376]{0,1:T(8,128)(2,1)}), bf16[1024,1376]{0,1:T(8,128)(2,1)}) %all-gather.19.cloned.1.call-update) | async-done | bytes 2818064 | tf_op jit(solution)/shard_map/all_gather | solution.py:196
  219.3 53.9 %all-gather.21.cloned.1.call-done = bf16[1024,1376]{0,1:T(8,128)(2,1)} async-done(((bf16[256,1376]{0,1:T(8,128)(2,1)}), bf16[1024,1376]{0,1:T(8,128)(2,1)}) %all-gather.21.cloned.1.call-update) | async-done | bytes 2818064 | tf_op jit(solution)/shard_map/all_gather | solution.py:197
  281.4 37.6 %all-reduce.17.cloned.1.call-done = f32[256,1024]{1,0:T(8,128)} async-done(((f32[256,1024]{1,0:T(8,128)}), f32[256,1024]{1,0:T(8,128)}) %all-reduce.17.cloned.1.call-update) | async-done | bytes 1048592 | tf_op jit(solution)/shard_map/psum | solution.py:167
  322.0 56.6 %all-gather.23.cloned.1.call-done = bf16[1376,1024]{1,0:T(8,128)(2,1)} async-done(((bf16[1376,256]{1,0:T(8,128)(2,1)}), bf16[1376,1024]{1,0:T(8,128)(2,1)}) %all-gather.23.cloned.1.call-update) | async-done | bytes 2818064 | tf_op jit(solution)/shard_map/all_gather | solution.py:267
  386.8 10.9 %all-gather.27.cloned.1.call-start = ((), (), s32[]{:S(2)}) async-start(), calls=%async_computation.24 | async-start | bytes 1966080 | tf_op jit(solution)/shard_map/all_gather | solution.py:62
  397.7 16.1 %all-reduce.19.cloned.1.call-done = bf16[256,1024]{1,0:T(8,128)(2,1)} async-done(((bf16[256,1024]{1,0:T(8,128)(2,1)}), bf16[256,1024]{1,0:T(8,128)(2,1)}) %all-reduce.19.cloned.1.call-update) | async-done | bytes 524304 | tf_op jit(solution)/shard_map/psum | solution.py:171
  427.0 5.2 all-gather.4
  452.1 18.1 %while.35 = (s32[]{:T(128)}, f32[1]{0:T(128)}, f32[1,8,273,64]{3,2,1,0:T(8,128)S(1)}, f32[1,8,273]{2,1,0:T(8,128)S(1)}, s32[]{:T(128)}, /*index=5*/bf16[4,1]{0,1...) while((s32[]{:T(128)}, f32[1]{0:T(128)}, ...), condition=%wide.region_14.15_spmd.clone, body=%wide.region_13.14_spmd.clone.sunk | while | flops 851772 | bytes 2538059 | solution.py:78
  502.6 21.3 %reduce-scatter.10.cloned.1.call-done = bf16[256,128]{1,0:T(8,128)(2,1)} async-done(((bf16[1024,128]{1,0:T(8,128)(2,1)}), bf16[256,128]{1,0:T(8,128)(2,1)}) %reduce-scatter.10.cloned.1.call-update) | async-done | bytes 65552 | tf_op jit(solution)/shard_map/reduce_scatter | solution.py:343
  524.0 28.3 %reduce-scatter.12.cloned.1.call-done = bf16[256,512]{1,0:T(8,128)(2,1)} async-done(((bf16[1024,512]{1,0:T(8,128)(2,1)}), bf16[256,512]{1,0:T(8,128)(2,1)}) %reduce-scatter.12.cloned.1.call-update) | async-done | bytes 262160 | tf_op jit(solution)/shard_map/reduce_scatter | solution.py:346
  552.3 56.0 %reduce-scatter.20.cloned.1.call-done = bf16[1376,256]{1,0:T(8,128)(2,1)} async-done(((bf16[1376,1024]{1,0:T(8,128)(2,1)}), bf16[1376,256]{1,0:T(8,128)(2,1)}) %reduce-scatter.20.cloned.1.call-update) | async-done | bytes 704528 | tf_op jit(solution)/shard_map/reduce_scatter | solution.py:361
  608.3 57.2 %reduce-scatter.16.cloned.1.call-done = bf16[256,1376]{0,1:T(8,128)(2,1)} async-done(((bf16[1024,1376]{0,1:T(8,128)(2,1)}), bf16[256,1376]{0,1:T(8,128)(2,1)}) %reduce-scatter.16.cloned.1.call-update) | async-done | bytes 704528 | tf_op jit(solution)/shard_map/reduce_scatter | solution.py:355
  665.4 57.2 %reduce-scatter.18.cloned.1.call-done = bf16[256,1376]{0,1:T(8,128)(2,1)} async-done(((bf16[1024,1376]{0,1:T(8,128)(2,1)}), bf16[256,1376]{0,1:T(8,128)(2,1)}) %reduce-scatter.18.cloned.1.call-update) | async-done | bytes 704528 | tf_op jit(solution)/shard_map/reduce_scatter | solution.py:358
  724.5 32.4 %all-reduce.4 = (f32[]{:T(128)}, f32[]{:T(128)}) all-reduce(f32[]{:T(128)} %get-tuple-element.393, f32[]{:T(128)} %convert_reduce_fusion), channel_id=1, replica_groups=mesh['fsdp'=4,'ctx'=4,'tp'=2] {'fsdp','ctx'}, use_global_device_ids=true, to_apply=%region_40.41 | all-reduce | flops 2 | bytes 16 | tf_op jit(solution)/shard_map/psum | solution.py:332
  759.6 8.4 %all-reduce.8 = (bf16[1024]{0:T(1024)(128)(2,1)S(1)}, bf16[1024]{0:T(1024)(128)(2,1)S(1)}) all-reduce(bf16[1024]{0:T(1024)(128)(2,1)S(1)} %get-tuple-element.344, bf16[1024]{0:T(1024)(128)(2,1)S(1)} %copy-done.57), channel_id=7, replica_groups=mesh['fsdp'=4,'ctx'=4,'tp'=2] {'fsdp'}, use_global_device_ids=true, to_apply=%region_20.21.clone | all-reduce | flops 2048 | bytes 8192
  768.2 6.3 all-reduce.5
  777.8 41.5 %all-reduce.23.cloned.1.call-done = (bf16[256,128]{1,0:T(8,128)(2,1)}, bf16[256,128]{1,0:T(8,128)(2,1)}, bf16[256,512]{1,0:T(8,128)(2,1)}, bf16[512,256]{1,0:T(8...) async-done(((bf16[256,128]{1,0:T(8,128)(2,1)}, bf16[256,128]{1,0:T(8,128)(2,1)}, bf16[256,512]{1,0:T(8,128)(2,1)}, ...) | async-done | bytes 2768912 | tf_op jit(solution)/shard_map/psum | solution.py:367
  (316 shorter events, 174.4 us)
Async XLA Ops:
  7.2 37.4 %all-gather.15.cloned.1.call-start = ((), (), s32[]{:S(2)}) async-start(), calls=%async_computation.7 | async-start | bytes 1310720 | tf_op jit(solution)/shard_map/all_gather | solution.py:193
  7.9 86.7 %all-gather.25.cloned.1.call-start = ((), (), s32[]{:S(2)}) async-start(), calls=%async_computation.23 | async-start | bytes 1966080 | tf_op jit(solution)/shard_map/all_gather | solution.py:40
  52.8 50.0 %all-gather.17.cloned.1.call-start = ((), (), s32[]{:S(2)}) async-start(), calls=%async_computation.8 | async-start | bytes 1310720 | tf_op jit(solution)/shard_map/all_gather | solution.py:194
  53.5 119.8 %all-reduce.15.cloned.1.call-start = ((), (), s32[]{:S(2)}) async-start(), calls=%async_computation.9 | async-start | bytes 2097152 | tf_op jit(solution)/shard_map/psum | solution.py:167
  95.0 328.2 %copy-start.59 = (f32[1,256]{1,0:T(1,128)}, f32[1,256]{1,0:T(1,128)S(1)}, u32[]{:S(2)}) copy-start(f32[1,256]{1,0:T(1,128)S(1)} %compare_convert_fusion) | copy-start | bytes 3076
  105.6 109.9 %all-gather.19.cloned.1.call-start = ((), (), s32[]{:S(2)}) async-start(), calls=%async_computation.10 | async-start | bytes 3522560 | tf_op jit(solution)/shard_map/all_gather | solution.py:196
  106.2 167.0 %all-gather.21.cloned.1.call-start = ((), (), s32[]{:S(2)}) async-start(), calls=%async_computation.11 | async-start | bytes 3522560 | tf_op jit(solution)/shard_map/all_gather | solution.py:197
  106.8 212.2 %all-reduce.17.cloned.1.call-start = ((), (), s32[]{:S(2)}) async-start(), calls=%async_computation.12 | async-start | bytes 2097152 | tf_op jit(solution)/shard_map/psum | solution.py:167
  106.8 18.8 %collective-permute-start = (bf16[1376,256]{1,0:T(8,128)(2,1)S(1)}, bf16[1376,256]{1,0:T(8,128)(2,1)S(1)}, u32[]{:S(2)}, u32[]{:S(2)}) collective-permute-start(bf16[1376,256]{1,0:T(8,128)(2,1)S(1)} %copy-done.22), channel_id=1, source_target_pairs={{0,8},{8,16},{16,24},{24,0},{1,9},{9,17},{17,25},{25,1},{2,10},{10... | collective-permute-start | bytes 2113544 | tf_op jit(solution)/shard_map/ppermute | solution.py:28
  109.4 52.3 %collective-permute-start.2 = (bf16[1376,256]{1,0:T(8,128)(2,1)S(1)}, bf16[1376,256]{1,0:T(8,128)(2,1)S(1)}, u32[]{:S(2)}, u32[]{:S(2)}) collective-permute-start(bf16[1376,256]{1,0:T(8,128)(2,1)S(1)} %copy-done.22), channel_id=1, source_target_pairs={{8,0},{16,8},{24,16},{0,24},{9,1},{17,9},{25,17},{1,25},{10,2},{18... | collective-permute-start | bytes 2113544 | tf_op jit(solution)/shard_map/ppermute | solution.py:30
  125.6 36.1 %collective-permute-start.1 = (bf16[1376,256]{1,0:T(8,128)(2,1)S(1)}, bf16[1376,256]{1,0:T(8,128)(2,1)}, u32[]{:S(2)}, u32[]{:S(2)}) collective-permute-start(bf16[1376,256]{1,0:T(8,128)(2,1)S(1)} %collective-permute-done), channel_id=1, source_target_pairs={{0,8},{8,16},{16,24},{24,0},{1,9},{9,17},{17,25},{25,1},{2,10},{10... | collective-permute-start | bytes 2113544 | tf_op jit(solution)/shard_map/ppermute | solution.py:28
  280.5 98.1 %all-gather.23.cloned.1.call-start = ((), (), s32[]{:S(2)}) async-start(), calls=%async_computation.13 | async-start | bytes 3522560 | tf_op jit(solution)/shard_map/all_gather | solution.py:267
  281.3 132.5 %all-reduce.19.cloned.1.call-start = ((), (), s32[]{:S(2)}) async-start(), calls=%async_computation.14 | async-start | bytes 1048576 | tf_op jit(solution)/shard_map/psum | solution.py:171
  386.8 65.2 %all-gather.27.cloned.1.call-start = ((), (), s32[]{:S(2)}) async-start(), calls=%async_computation.24 | async-start | bytes 1966080 | tf_op jit(solution)/shard_map/all_gather | solution.py:62
  432.3 66.1 %reduce-scatter.8.cloned.1.call-start = ((), (), s32[]{:S(2)}) async-start(), calls=%async_computation.16 | async-start | bytes 327680 | tf_op jit(solution)/shard_map/reduce_scatter | solution.py:340
  442.7 60.0 %reduce-scatter.14.cloned.1.call-start = ((), (), s32[]{:S(2)}) async-start(), calls=%async_computation.19 | async-start | bytes 1310720 | tf_op jit(solution)/shard_map/reduce_scatter | solution.py:349
  449.0 75.0 %reduce-scatter.10.cloned.1.call-start = ((), (), s32[]{:S(2)}) async-start(), calls=%async_computation.17 | async-start | bytes 327680 | tf_op jit(solution)/shard_map/reduce_scatter | solution.py:343
  478.3 74.0 %reduce-scatter.12.cloned.1.call-start = ((), (), s32[]{:S(2)}) async-start(), calls=%async_computation.18 | async-start | bytes 1310720 | tf_op jit(solution)/shard_map/reduce_scatter | solution.py:346
  484.9 123.4 %reduce-scatter.20.cloned.1.call-start = ((), (), s32[]{:S(2)}) async-start(), calls=%async_computation.22 | async-start | bytes 3522560 | tf_op jit(solution)/shard_map/reduce_scatter | solution.py:361
  487.4 178.0 %reduce-scatter.16.cloned.1.call-start = ((), (), s32[]{:S(2)}) async-start(), calls=%async_computation.20 | async-start | bytes 3522560 | tf_op jit(solution)/shard_map/reduce_scatter | solution.py:355
  491.2 231.5 %reduce-scatter.18.cloned.1.call-start = ((), (), s32[]{:S(2)}) async-start(), calls=%async_computation.21 | async-start | bytes 3522560 | tf_op jit(solution)/shard_map/reduce_scatter | solution.py:358
  494.8 263.5 %all-reduce.21.cloned.1.call-start = ((), (), s32[]{:S(2)}) async-start(), calls=%async_computation.15 | async-start | bytes 1048576 | tf_op jit(solution)/shard_map/psum | solution.py:171
  498.3 277.4 %copy-start.58 = (f32[256]{0:T(256)S(1)}, f32[256]{0:T(256)}, u32[]{:S(2)}) copy-start(f32[256]{0:T(256)} %get-tuple-element.406) | copy-start | bytes 3076
  498.3 321.0 %all-reduce.23.cloned.1.call-start = ((), (), s32[]{:S(2)}) async-start(), calls=%async_computation.25 | async-start | bytes 5537792 | tf_op jit(solution)/shard_map/psum | solution.py:367
  (70 other events, 1122.4 us)
Sparse Core Ops, SparseCore 0:
  9.6 34.3 all-gather.14
  52.9 18.2 all-gather.24
  72.8 29.9 all-gather.16
  105.7 50.2 all-reduce.14
  157.4 58.0 all-gather.18
  216.9 56.2 all-gather.20
  280.7 38.2 all-reduce.16
  320.5 58.0 all-gather.22
  386.9 26.8 all-reduce.18
  432.4 19.6 all-gather.26
  454.3 19.9 reduce-scatter.7
  477.1 25.5 reduce-scatter.13
  505.5 18.4 reduce-scatter.9
  526.7 25.5 reduce-scatter.11
  554.4 53.7 reduce-scatter.19
  610.4 54.9 reduce-scatter.15
  667.6 54.9 reduce-scatter.17
  725.4 28.3 all-reduce.20
  756.6 62.6 all-reduce.22
